TPU v7x, 32 devices: a whole 2x2x4 slice. The times are simulated.
32 devices in a mesh: gx: 8 (over z, x), gy: 4 (over y, core).
Axes of the slice: x: 2, y: 2, z: 4, core: 2. Of those that a mesh axis runs over, the one named last changes fastest.
Arguments:
- mode_fields: float32 [32, 512, 1024], P(None, 'gx', 'gy'), may hold values from -60 to 60, as said below
- conductance: float32 [512, 1024], P('gx', 'gy'), may hold values from 0.5 to 2
- potential: float32 [512, 1024], P('gx', 'gy'), may hold values from 0.25 to 4
Outputs:
- basis_field: float32 [128, 512, 1024], P(None, 'gx', 'gy')
- scaled_factor: float32 [128, 128], replicated
Inputs may be any that keep to these rules, and one draw needn't show every extreme that they name: `mode_fields`: Real-valued mode amplitudes.
All inputs are finite; a program needn't handle non-finite values.
Results may differ from a plain program's by a relative error of at most 0.0003.
Values sent between devices are 32-bit elements; how exact they have to be, the bound alone decides.
A program may use at most 64 MiB of HBM per device.

v0:
```python
import jax
import jax.numpy as jnp
from jax import lax
from jax.sharding import PartitionSpec as P


def padded_2(value, sides, width):
    for axis, dim in sides:
        peers, length = (lax.axis_size(axis), value.shape[dim])
        up = [(i, (i + 1) % peers) for i in range(peers - 1)]
        down = [(j, i) for i, j in up]
        last = lax.slice_in_dim(value, length - width, length, axis=dim)
        first = lax.slice_in_dim(value, 0, width, axis=dim)
        before = lax.ppermute(last, axis, up)
        after = lax.ppermute(first, axis, down)
        value = jnp.concatenate([before, value, after], axis=dim)
    return value


def build_columns(fields, conduct, potential):
    center = fields[:, 1:-1, 1:-1]
    k_mid = conduct[1:-1, 1:-1]
    x_plus = 0.5 * (k_mid + conduct[2:, 1:-1])
    x_minus = 0.5 * (k_mid + conduct[:-2, 1:-1])
    y_plus = 0.5 * (k_mid + conduct[1:-1, 2:])
    y_minus = 0.5 * (k_mid + conduct[1:-1, :-2])
    along_x = x_plus * (center - fields[:, 2:, 1:-1]) + x_minus * (center - fields[:, :-2, 1:-1])
    along_y = y_plus * (center - fields[:, 1:-1, 2:]) + y_minus * (center - fields[:, 1:-1, :-2])
    react = potential * center
    stacked = jnp.concatenate([center, along_x, along_y, react], 0)
    return stacked.reshape(stacked.shape[0], -1)


def inner_products(matrix, cell_count):
    return jnp.dot(matrix, matrix.T, precision=lax.Precision.HIGHEST) / cell_count


def on_device(mode_fields, conductance, potential):
    modes_count = mode_fields.shape[0]
    rows_here = mode_fields.shape[1]
    cols_here = mode_fields.shape[2]
    stacked = jnp.concatenate([mode_fields, conductance[None]], 0)
    padded = padded_2(stacked, (("gx", 1), ("gy", 2)), 1)
    matrix = build_columns(padded[:modes_count], padded[modes_count], potential)
    cell_count = float(rows_here * cols_here * lax.axis_size("gx") * lax.axis_size("gy"))
    gram_total = lax.psum(inner_products(matrix, cell_count), ("gx", "gy"))
    lower_tri = jnp.linalg.cholesky(gram_total)
    basis_flat = jax.scipy.linalg.solve_triangular(lower_tri, matrix, lower=True)
    basis_field = basis_flat.reshape(basis_flat.shape[0], rows_here, cols_here)
    return (basis_field, lower_tri.T)


def solution(mesh):
    placed = (P(None, "gx", "gy"), P("gx", "gy"), P("gx", "gy"))
    return jax.shard_map(
        on_device, mesh=mesh, in_specs=placed, out_specs=(P(None, "gx", "gy"), P()), check_vma=False
    )
```

profile of v0, /device:TPU:1, one launch (start us, length us, event | category | flops | bytes accessed | tf_op | source)
XLA Modules:
  0.0 232.6 jit_solution(10538956578714779694)
XLA Ops:
  7.2 0.9 broadcast_in_dim.3
  8.1 5.0 %fusion.22 = (f32[32,64,256]{2,0,1:T(8,128)}, f32[33,64,256]{2,0,1:T(8,128)S(1)}, f32[32,64,256]{2,0,1:T(8,128)}) fusion(f32[32,64,256]{2,1,0:T(8,128)} %param.3, f32[64,256]{1,0:T(8,128)} %param.5), kind=kLoop, calls=%fused_computation.51 | loop fusion | flops 524287 | bytes 8454144 | tf_op args[0]
  13.1 0.9 dynamic-update-slice.4
  14.0 3.9 %collective-permute-start = (f32[33,1,256]{2,0,1:T(8,128)S(1)}, f32[33,1,256]{2,0,1:T(8,128)S(1)}, u32[]{:S(2)}, u32[]{:S(2)}) collective-permute-start(f32[33,1,256]{2,0,1:T(8,128)S(1)} %get-tuple-element.12), channel_id=1, source_target_pairs={{0,4},{4,8},{8,12},{12,16},{16,20},{20,24},{24,28},{1,5},{5,9},{9,... | collective-permute-start | bytes 101384 | tf_op jit(solution)/shard_map/ppermute | solution.py:14
  17.9 1.3 collective-permute-start.1
  19.2 3.4 %collective-permute-done.1 = f32[33,1,256]{2,0,1:T(8,128)S(1)} collective-permute-done((f32[33,1,256]{2,0,1:T(8,128)S(1)}, f32[33,1,256]{2,0,1:T(8,128)S(1)}, u32[]{:S(2)}, u32[]{:S(2)}) %collective-permute-start.1) | collective-permute-done | bytes 33824 | tf_op jit(solution)/shard_map/ppermute | solution.py:15
  22.7 0.2 pad_maximum_fusion.1
  22.8 1.9 fusion.20
  24.8 1.8 copy.32
  26.6 4.0 %collective-permute-start.3 = (f32[33,66,1]{1,2,0:T(1,128)S(1)}, f32[33,66,1]{1,2,0:T(1,128)S(1)}, u32[]{:S(2)}, u32[]{:S(2)}) collective-permute-start(f32[33,66,1]{1,2,0:T(1,128)S(1)} %copy.32), channel_id=1, source_target_pairs={{1,0},{2,1},{3,2},{5,4},{6,5},{7,6},{9,8},{10,9},{11,10},{13,12},{... | collective-permute-start | bytes 26144 | tf_op jit(solution)/shard_map/ppermute | solution.py:15
  30.6 1.8 copy.31
  32.4 3.1 %collective-permute-start.2 = (f32[33,66,1]{1,2,0:T(1,128)S(1)}, f32[33,66,1]{1,2,0:T(1,128)S(1)}, u32[]{:S(2)}, u32[]{:S(2)}) collective-permute-start(f32[33,66,1]{1,2,0:T(1,128)S(1)} %copy.31), channel_id=1, source_target_pairs={{0,1},{1,2},{2,3},{4,5},{5,6},{6,7},{8,9},{9,10},{10,11},{12,13},{... | collective-permute-start | bytes 26144 | tf_op jit(solution)/shard_map/ppermute | solution.py:14
  35.4 1.7 copy.34
  37.1 1.7 copy.33
  38.8 1.5 pad_maximum_fusion.10
  40.3 0.1 fusion.16
  40.5 0.2 copy-done.1
  40.7 0.7 copy-done.2
  41.3 7.0 %fusion.9 = (f32[32,64,256]{2,0,1:T(8,128)}, f32[32,64,256]{2,0,1:T(8,128)}) fusion(f32[33,64,256]{2,0,1:T(8,128)S(1)} %dynamic-update-slice.4, f32[33,1,256]{2,0,1:T(8,128)S(1)} %collective-permute-done, f32[33,1,256]{2,0,1:T(8,128)S(1)} %collective-permute-done.1, f32[64,256]{1,0:T(8,128)S(1)} %get-tuple-element.19, f32[64,256]{1,0:T(8,128)S(1)} %get-tuple-element.17, ...), kind=kLoop, calls=%fused_computation.18 | loop fusion | flops 9437184 | bytes 8801296 | tf_op jit(solution)/shard_map/add | solution.py:27
  48.3 10.7 %fusion.12 = f32[128,128]{0,1:T(8,128)} fusion(f32[32,64,256]{2,0,1:T(8,128)} %get-tuple-element.16, f32[32,64,256]{2,0,1:T(8,128)} %get-tuple-element.9, f32[32,64,256]{2,0,1:T(8,128)} %get-tuple-element.8, f32[32,64,256]{2,0,1:T(8,128)S(1)} %copy-done.3), kind=kOutput, calls=%fused_computation.23 | convolution fusion | flops 3227533312 | bytes 8454144 | tf_op jit(solution)/shard_map/dot_general | solution.py:35
  59.0 5.7 %pad_maximum_fusion = f32[128,64,256]{2,0,1:T(8,128)} fusion(f32[32,64,256]{2,0,1:T(8,128)} %get-tuple-element.16, f32[32,64,256]{2,0,1:T(8,128)} %get-tuple-element.9, f32[32,64,256]{2,0,1:T(8,128)} %get-tuple-element.8, f32[32,64,256]{2,0,1:T(8,128)S(1)} %copy-done.4), kind=kLoop, calls=%fused_computation | loop fusion | flops 6291456 | bytes 16777216 | tf_op jit(solution)/shard_map/concatenate | solution.py:30
  64.7 9.0 %copy.45 = f32[128,64,256]{0,2,1:T(8,128)} copy(f32[128,64,256]{2,0,1:T(8,128)} %pad_maximum_fusion) | data formatting | bytes 16777216 | tf_op jit(solution)/shard_map/concatenate | solution.py:30
  73.7 107.6 %all-reduce.2.cloned.1.call-done = f32[128,128]{0,1:T(8,128)} async-done(((f32[128,128]{0,1:T(8,128)}), f32[128,128]{0,1:T(8,128)}) %all-reduce.2.cloned.1.call-update) | async-done | bytes 65552 | tf_op jit(solution)/shard_map/psum | solution.py:46
  181.3 0.9 copy.44
  182.3 0.9 fusion.18
  183.1 11.7 %cholesky.16 = f32[128,128]{1,0:T(8,128)S(1)} custom-call(f32[128,128]{1,0:T(8,128)S(1)} %fusion.18), custom_call_target="Cholesky" | custom-call | tf_op jit(solution)/shard_map/jit(cholesky)/cholesky | solution.py:47
  194.9 0.6 compare_reduce_fusion
  195.5 0.7 fusion.19
  196.2 0.7 copy.48
  196.9 9.8 %custom-call.7 = f32[1,128,128]{1,2,0:T(8,128)S(1)} custom-call(f32[1,128,128]{2,1,0:T(8,128)S(1)} %get-tuple-element.22), custom_call_target="InvertDiagBlocksLowerTriangular" | custom-call | tf_op jit(solution)/shard_map/jit(_solve_triangular)/triangular_solve | solution.py:48
  206.7 10.7 %fusion = f32[128,64,256]{2,0,1:T(8,128)S(1)} fusion(f32[128,64,256]{0,2,1:T(8,128)} %copy.45, f32[1,128,128]{1,2,0:T(8,128)S(1)} %custom-call.7), kind=kOutput, calls=%fused_computation.1 | convolution fusion | flops 3221225472 | bytes 16842752 | tf_op jit(solution)/shard_map/jit(_solve_triangular)/triangular_solve | solution.py:48
  217.5 8.3 %copy.47 = f32[128,64,256]{2,1,0:T(8,128)} copy(f32[128,64,256]{2,0,1:T(8,128)S(1)} %fusion) | data formatting | bytes 16777216
  (16 shorter events, 0.1 us)
Async XLA Ops:
  7.2 174.2 %all-reduce.2.cloned.1.call-start = ((), (), s32[]{:S(2)}) async-start(), calls=%async_computation | async-start | bytes 131072 | tf_op jit(solution)/shard_map/psum | solution.py:46
  14.0 5.2 %collective-permute-start = (f32[33,1,256]{2,0,1:T(8,128)S(1)}, f32[33,1,256]{2,0,1:T(8,128)S(1)}, u32[]{:S(2)}, u32[]{:S(2)}) collective-permute-start(f32[33,1,256]{2,0,1:T(8,128)S(1)} %get-tuple-element.12), channel_id=1, source_target_pairs={{0,4},{4,8},{8,12},{12,16},{16,20},{20,24},{24,28},{1,5},{5,9},{9,... | collective-permute-start | bytes 101384 | tf_op jit(solution)/shard_map/ppermute | solution.py:14
  17.9 4.7 %collective-permute-start.1 = (f32[33,1,256]{2,0,1:T(8,128)S(1)}, f32[33,1,256]{2,0,1:T(8,128)S(1)}, u32[]{:S(2)}, u32[]{:S(2)}) collective-permute-start(f32[33,1,256]{2,0,1:T(8,128)S(1)} %get-tuple-element.13), channel_id=1, source_target_pairs={{4,0},{8,4},{12,8},{16,12},{20,16},{24,20},{28,24},{5,1},{9,5},{13... | collective-permute-start | bytes 101384 | tf_op jit(solution)/shard_map/ppermute | solution.py:15
  26.6 8.9 %collective-permute-start.3 = (f32[33,66,1]{1,2,0:T(1,128)S(1)}, f32[33,66,1]{1,2,0:T(1,128)S(1)}, u32[]{:S(2)}, u32[]{:S(2)}) collective-permute-start(f32[33,66,1]{1,2,0:T(1,128)S(1)} %copy.32), channel_id=1, source_target_pairs={{1,0},{2,1},{3,2},{5,4},{6,5},{7,6},{9,8},{10,9},{11,10},{13,12},{... | collective-permute-start | bytes 26144 | tf_op jit(solution)/shard_map/ppermute | solution.py:15
  32.4 4.7 %collective-permute-start.2 = (f32[33,66,1]{1,2,0:T(1,128)S(1)}, f32[33,66,1]{1,2,0:T(1,128)S(1)}, u32[]{:S(2)}, u32[]{:S(2)}) collective-permute-start(f32[33,66,1]{1,2,0:T(1,128)S(1)} %copy.31), channel_id=1, source_target_pairs={{0,1},{1,2},{2,3},{4,5},{5,6},{6,7},{8,9},{9,10},{10,11},{12,13},{... | collective-permute-start | bytes 26144 | tf_op jit(solution)/shard_map/ppermute | solution.py:14
  38.8 1.7 copy-start
  38.8 1.9 copy-start.1
  38.8 2.6 %copy-start.2 = (f32[32,64,256]{2,1,0:T(8,128)S(1)}, f32[32,64,256]{2,1,0:T(8,128)}, u32[]{:S(2)}) copy-start(f32[32,64,256]{2,1,0:T(8,128)} %param.3) | copy-start | bytes 6291460
  41.3 7.0 %copy-start.3 = (f32[32,64,256]{2,0,1:T(8,128)S(1)}, f32[32,64,256]{2,0,1:T(8,128)}, u32[]{:S(2)}) copy-start(f32[32,64,256]{2,0,1:T(8,128)} %get-tuple-element.14) | copy-start | bytes 6291460
  48.3 10.7 %copy-start.4 = (f32[32,64,256]{2,0,1:T(8,128)S(1)}, f32[32,64,256]{2,0,1:T(8,128)}, u32[]{:S(2)}) copy-start(f32[32,64,256]{2,0,1:T(8,128)} %get-tuple-element.14) | copy-start | bytes 6291460
Sparse Core Ops, SparseCore 0:
  59.2 122.1 all-reduce.1
where the time goes:
time: 233 us
  waiting for transfers between devices  111 us (48%)
  other arithmetic  43.2 us (19%)
  local copies, waits for them, and re-layouts  30.4 us (13%)
  matrix products  21.4 us (9%)
  between operations  14.2 us (6%)
  starting transfers between devices  12.3 us (5%)
    psum x1, waiting for transfers between devices, on_device(): gram_total = lax.psum(inner_products(matrix, cell_count), ('gx', 'gy'))  108 us
    another operation x3, other arithmetic, on_device(): lower_tri = jnp.linalg.cholesky(gram_total)  12.4 us
    another operation x1, matrix products, on_device(): jax.scipy.linalg.solve_triangular(lower_tri, matrix, lower=True)  10.7 us
    dot_general x1, matrix products, inner_products(): jnp.dot(matrix, matrix.T, precision=lax.Precision.HIGHEST) / cell_count  10.7 us
    unnamed x13, local copies, waits for them, and re-layouts  9.88 us
    another operation x1, other arithmetic, on_device(): jax.scipy.linalg.solve_triangular(lower_tri, matrix, lower=True)  9.81 us
    concatenate x1, local copies, waits for them, and re-layouts, build_columns(): stacked = jnp.concatenate([center, along_x, along_y, react], 0)  9.01 us
    ppermute x2, starting transfers between devices, padded_2(): before = lax.ppermute(last, axis, up)  6.99 us
  transfers between devices with their start and end apart: 5, of which 2 were waited for; matrix products, arithmetic and copies ran while one was open for 8% of the time, Pallas kernels for 0%

commit v1 on v0

--- a/solution.py
+++ b/solution.py
@@ -43,7 +43,8 @@
     padded = padded_2(stacked, (("gx", 1), ("gy", 2)), 1)
     matrix = build_columns(padded[:modes_count], padded[modes_count], potential)
     cell_count = float(rows_here * cols_here * lax.axis_size("gx") * lax.axis_size("gy"))
-    gram_total = lax.psum(inner_products(matrix, cell_count), ("gx", "gy"))
+    inner = lax.psum(inner_products(matrix, cell_count), "gx")
+    gram_total = lax.psum(inner, "gy")
     lower_tri = jnp.linalg.cholesky(gram_total)
     basis_flat = jax.scipy.linalg.solve_triangular(lower_tri, matrix, lower=True)
     basis_field = basis_flat.reshape(basis_flat.shape[0], rows_here, cols_here)

time: 233 us -> 216 us (0.927); the launches traced: 233 us -> 213 us
  waiting for transfers between devices: 111 us -> 91.1 us
    psum x1 -> x2, waiting for transfers between devices: 108 us -> 87.6 us  [the longest x1 68.2 us: on_device(): inner = lax.psum(inner_products(matrix, cell_count), 'gx')]
  transfers between devices with their start and end apart: 5 -> 6, of which waited for: 2 -> 3; matrix products, arithmetic and copies ran while one was open for 8% -> 9% of each run, Pallas kernels for 0% -> 0%
where the time goes in v1:
time: 216 us; the launch traced here: 213 us
  waiting for transfers between devices  91.1 us (42%)
  other arithmetic  43.2 us (20%)
  local copies, waits for them, and re-layouts  30.4 us (14%)
  matrix products  21.4 us (10%)
  between operations  14.2 us (7%)
  starting transfers between devices  12.6 us (6%)
    psum x1, waiting for transfers between devices, on_device(): inner = lax.psum(inner_products(matrix, cell_count), 'gx')  68.2 us
    psum x1, waiting for transfers between devices, on_device(): gram_total = lax.psum(inner, 'gy')  19.5 us
    another operation x3, other arithmetic, on_device(): lower_tri = jnp.linalg.cholesky(gram_total)  12.4 us
    another operation x1, matrix products, on_device(): jax.scipy.linalg.solve_triangular(lower_tri, matrix, lower=True)  10.7 us
    dot_general x1, matrix products, inner_products(): jnp.dot(matrix, matrix.T, precision=lax.Precision.HIGHEST) / cell_count  10.7 us
    unnamed x13, local copies, waits for them, and re-layouts  9.88 us
    another operation x1, other arithmetic, on_device(): jax.scipy.linalg.solve_triangular(lower_tri, matrix, lower=True)  9.81 us
    concatenate x1, local copies, waits for them, and re-layouts, build_columns(): stacked = jnp.concatenate([center, along_x, along_y, react], 0)  9.01 us
  transfers between devices with their start and end apart: 6, of which 3 were waited for; matrix products, arithmetic and copies ran while one was open for 9% of the time, Pallas kernels for 0%

profile of v1, /device:TPU:1, one launch (start us, length us, event | category | flops | bytes accessed | tf_op | source)
XLA Modules:
  0.0 212.9 jit_solution(1584138746007479680)
XLA Ops:
  7.2 0.9 broadcast_in_dim.3
  8.1 5.0 %fusion.22 = (f32[32,64,256]{2,0,1:T(8,128)}, f32[33,64,256]{2,0,1:T(8,128)S(1)}, f32[32,64,256]{2,0,1:T(8,128)}) fusion(f32[32,64,256]{2,1,0:T(8,128)} %param.3, f32[64,256]{1,0:T(8,128)} %param.5), kind=kLoop, calls=%fused_computation.51 | loop fusion | flops 524287 | bytes 8454144 | tf_op args[0]
  13.1 0.9 dynamic-update-slice.4
  14.0 3.9 %collective-permute-start = (f32[33,1,256]{2,0,1:T(8,128)S(1)}, f32[33,1,256]{2,0,1:T(8,128)S(1)}, u32[]{:S(2)}, u32[]{:S(2)}) collective-permute-start(f32[33,1,256]{2,0,1:T(8,128)S(1)} %get-tuple-element.12), channel_id=1, source_target_pairs={{0,4},{4,8},{8,12},{12,16},{16,20},{20,24},{24,28},{1,5},{5,9},{9,... | collective-permute-start | bytes 101384 | tf_op jit(solution)/shard_map/ppermute | solution.py:14
  17.9 1.3 collective-permute-start.1
  19.2 3.4 %collective-permute-done.1 = f32[33,1,256]{2,0,1:T(8,128)S(1)} collective-permute-done((f32[33,1,256]{2,0,1:T(8,128)S(1)}, f32[33,1,256]{2,0,1:T(8,128)S(1)}, u32[]{:S(2)}, u32[]{:S(2)}) %collective-permute-start.1) | collective-permute-done | bytes 33824 | tf_op jit(solution)/shard_map/ppermute | solution.py:15
  22.8 1.9 fusion.20
  24.8 1.8 copy.32
  26.6 4.0 %collective-permute-start.3 = (f32[33,66,1]{1,2,0:T(1,128)S(1)}, f32[33,66,1]{1,2,0:T(1,128)S(1)}, u32[]{:S(2)}, u32[]{:S(2)}) collective-permute-start(f32[33,66,1]{1,2,0:T(1,128)S(1)} %copy.32), channel_id=1, source_target_pairs={{1,0},{2,1},{3,2},{5,4},{6,5},{7,6},{9,8},{10,9},{11,10},{13,12},{... | collective-permute-start | bytes 26144 | tf_op jit(solution)/shard_map/ppermute | solution.py:15
  30.6 1.8 copy.31
  32.4 3.1 %collective-permute-start.2 = (f32[33,66,1]{1,2,0:T(1,128)S(1)}, f32[33,66,1]{1,2,0:T(1,128)S(1)}, u32[]{:S(2)}, u32[]{:S(2)}) collective-permute-start(f32[33,66,1]{1,2,0:T(1,128)S(1)} %copy.31), channel_id=1, source_target_pairs={{0,1},{1,2},{2,3},{4,5},{5,6},{6,7},{8,9},{9,10},{10,11},{12,13},{... | collective-permute-start | bytes 26144 | tf_op jit(solution)/shard_map/ppermute | solution.py:14
  35.4 1.7 copy.34
  37.1 1.7 copy.33
  38.8 1.5 pad_maximum_fusion.10
  40.5 0.2 copy-done.1
  40.7 0.7 copy-done.2
  41.3 7.0 %fusion.9 = (f32[32,64,256]{2,0,1:T(8,128)}, f32[32,64,256]{2,0,1:T(8,128)}) fusion(f32[33,64,256]{2,0,1:T(8,128)S(1)} %dynamic-update-slice.4, f32[33,1,256]{2,0,1:T(8,128)S(1)} %collective-permute-done, f32[33,1,256]{2,0,1:T(8,128)S(1)} %collective-permute-done.1, f32[64,256]{1,0:T(8,128)S(1)} %get-tuple-element.19, f32[64,256]{1,0:T(8,128)S(1)} %get-tuple-element.17, ...), kind=kLoop, calls=%fused_computation.18 | loop fusion | flops 9437184 | bytes 8801296 | tf_op jit(solution)/shard_map/add | solution.py:27
  48.3 10.7 %fusion.12 = f32[128,128]{0,1:T(8,128)} fusion(f32[32,64,256]{2,0,1:T(8,128)} %get-tuple-element.16, f32[32,64,256]{2,0,1:T(8,128)} %get-tuple-element.9, f32[32,64,256]{2,0,1:T(8,128)} %get-tuple-element.8, f32[32,64,256]{2,0,1:T(8,128)S(1)} %copy-done.3), kind=kOutput, calls=%fused_computation.23 | convolution fusion | flops 3227533312 | bytes 8454144 | tf_op jit(solution)/shard_map/dot_general | solution.py:35
  59.0 0.2 all-reduce.5.cloned.1.call-start
  59.3 68.2 %all-reduce.3.cloned.1.call-done = f32[128,128]{0,1:T(8,128)} async-done(((f32[128,128]{0,1:T(8,128)}), f32[128,128]{0,1:T(8,128)}) %all-reduce.3.cloned.1.call-update) | async-done | bytes 65552 | tf_op jit(solution)/shard_map/psum | solution.py:46
  127.5 5.7 %pad_maximum_fusion = f32[128,64,256]{2,0,1:T(8,128)} fusion(f32[32,64,256]{2,0,1:T(8,128)} %get-tuple-element.16, f32[32,64,256]{2,0,1:T(8,128)} %get-tuple-element.9, f32[32,64,256]{2,0,1:T(8,128)} %get-tuple-element.8, f32[32,64,256]{2,0,1:T(8,128)S(1)} %copy-done.4), kind=kLoop, calls=%fused_computation | loop fusion | flops 6291456 | bytes 16777216 | tf_op jit(solution)/shard_map/concatenate | solution.py:30
  133.2 9.0 %copy.45 = f32[128,64,256]{0,2,1:T(8,128)} copy(f32[128,64,256]{2,0,1:T(8,128)} %pad_maximum_fusion) | data formatting | bytes 16777216 | tf_op jit(solution)/shard_map/concatenate | solution.py:30
  142.2 19.5 %all-reduce.5.cloned.1.call-done = f32[128,128]{0,1:T(8,128)} async-done(((f32[128,128]{0,1:T(8,128)}), f32[128,128]{0,1:T(8,128)}) %all-reduce.5.cloned.1.call-update) | async-done | bytes 65552 | tf_op jit(solution)/shard_map/psum | solution.py:47
  161.7 0.9 copy.44
  162.6 0.9 fusion.18
  163.4 11.7 %cholesky.16 = f32[128,128]{1,0:T(8,128)S(1)} custom-call(f32[128,128]{1,0:T(8,128)S(1)} %fusion.18), custom_call_target="Cholesky" | custom-call | tf_op jit(solution)/shard_map/jit(cholesky)/cholesky | solution.py:48
  175.2 0.6 compare_reduce_fusion
  175.8 0.7 fusion.19
  176.5 0.7 copy.48
  177.2 9.8 %custom-call.7 = f32[1,128,128]{1,2,0:T(8,128)S(1)} custom-call(f32[1,128,128]{2,1,0:T(8,128)S(1)} %get-tuple-element.22), custom_call_target="InvertDiagBlocksLowerTriangular" | custom-call | tf_op jit(solution)/shard_map/jit(_solve_triangular)/triangular_solve | solution.py:49
  187.0 10.7 %fusion = f32[128,64,256]{2,0,1:T(8,128)S(1)} fusion(f32[128,64,256]{0,2,1:T(8,128)} %copy.45, f32[1,128,128]{1,2,0:T(8,128)S(1)} %custom-call.7), kind=kOutput, calls=%fused_computation.1 | convolution fusion | flops 3221225472 | bytes 16842752 | tf_op jit(solution)/shard_map/jit(_solve_triangular)/triangular_solve | solution.py:49
  197.8 8.3 %copy.47 = f32[128,64,256]{2,1,0:T(8,128)} copy(f32[128,64,256]{2,0,1:T(8,128)S(1)} %fusion) | data formatting | bytes 16777216
  (19 shorter events, 0.5 us)
Async XLA Ops:
  7.2 120.3 %all-reduce.3.cloned.1.call-start = ((), (), s32[]{:S(2)}) async-start(), calls=%async_computation | async-start | bytes 131072 | tf_op jit(solution)/shard_map/psum | solution.py:46
  14.0 5.2 %collective-permute-start = (f32[33,1,256]{2,0,1:T(8,128)S(1)}, f32[33,1,256]{2,0,1:T(8,128)S(1)}, u32[]{:S(2)}, u32[]{:S(2)}) collective-permute-start(f32[33,1,256]{2,0,1:T(8,128)S(1)} %get-tuple-element.12), channel_id=1, source_target_pairs={{0,4},{4,8},{8,12},{12,16},{16,20},{20,24},{24,28},{1,5},{5,9},{9,... | collective-permute-start | bytes 101384 | tf_op jit(solution)/shard_map/ppermute | solution.py:14
  17.9 4.7 %collective-permute-start.1 = (f32[33,1,256]{2,0,1:T(8,128)S(1)}, f32[33,1,256]{2,0,1:T(8,128)S(1)}, u32[]{:S(2)}, u32[]{:S(2)}) collective-permute-start(f32[33,1,256]{2,0,1:T(8,128)S(1)} %get-tuple-element.13), channel_id=1, source_target_pairs={{4,0},{8,4},{12,8},{16,12},{20,16},{24,20},{28,24},{5,1},{9,5},{13... | collective-permute-start | bytes 101384 | tf_op jit(solution)/shard_map/ppermute | solution.py:15
  26.6 8.9 %collective-permute-start.3 = (f32[33,66,1]{1,2,0:T(1,128)S(1)}, f32[33,66,1]{1,2,0:T(1,128)S(1)}, u32[]{:S(2)}, u32[]{:S(2)}) collective-permute-start(f32[33,66,1]{1,2,0:T(1,128)S(1)} %copy.32), channel_id=1, source_target_pairs={{1,0},{2,1},{3,2},{5,4},{6,5},{7,6},{9,8},{10,9},{11,10},{13,12},{... | collective-permute-start | bytes 26144 | tf_op jit(solution)/shard_map/ppermute | solution.py:15
  32.4 4.7 %collective-permute-start.2 = (f32[33,66,1]{1,2,0:T(1,128)S(1)}, f32[33,66,1]{1,2,0:T(1,128)S(1)}, u32[]{:S(2)}, u32[]{:S(2)}) collective-permute-start(f32[33,66,1]{1,2,0:T(1,128)S(1)} %copy.31), channel_id=1, source_target_pairs={{0,1},{1,2},{2,3},{4,5},{5,6},{6,7},{8,9},{9,10},{10,11},{12,13},{... | collective-permute-start | bytes 26144 | tf_op jit(solution)/shard_map/ppermute | solution.py:14
  38.8 1.7 copy-start
  38.8 1.9 copy-start.1
  38.8 2.6 %copy-start.2 = (f32[32,64,256]{2,1,0:T(8,128)S(1)}, f32[32,64,256]{2,1,0:T(8,128)}, u32[]{:S(2)}) copy-start(f32[32,64,256]{2,1,0:T(8,128)} %param.3) | copy-start | bytes 6291460
  41.3 7.0 %copy-start.3 = (f32[32,64,256]{2,0,1:T(8,128)S(1)}, f32[32,64,256]{2,0,1:T(8,128)}, u32[]{:S(2)}) copy-start(f32[32,64,256]{2,0,1:T(8,128)} %get-tuple-element.14) | copy-start | bytes 6291460
  48.3 79.1 %copy-start.4 = (f32[32,64,256]{2,0,1:T(8,128)S(1)}, f32[32,64,256]{2,0,1:T(8,128)}, u32[]{:S(2)}) copy-start(f32[32,64,256]{2,0,1:T(8,128)} %get-tuple-element.14) | copy-start | bytes 6291460
  59.0 102.6 %all-reduce.5.cloned.1.call-start = ((), (), s32[]{:S(2)}) async-start(), calls=%async_computation.1 | async-start | bytes 131072 | tf_op jit(solution)/shard_map/psum | solution.py:47
Sparse Core Ops, SparseCore 0:
  59.2 68.2 all-reduce.2
  129.7 31.8 all-reduce.4
